TPU v7x, 256 devices: a whole 4x4x8 slice. The times are simulated.
256 devices in a mesh: grp: 16 (over y, z_hi, core), dp: 16 (over z_lo, x).
Axes of the slice: x: 4, y: 4, z: 8 (z_hi: 2, z_lo: 4; z = z_hi * 4 + z_lo), core: 2. Of those that a mesh axis runs over, the one named last changes fastest.
Arguments:
- tokens: bfloat16 [16, 2048, 2048], P('grp', 'dp'), may hold values from -6 to 6
- hidden_grad: bfloat16 [16, 2048, 6144], P('grp', 'dp'), may hold values from -6 to 6
- w_gate: bfloat16 [16, 2048, 6144], P('grp', None, 'dp'), may hold values from -6 to 6
- w_up: bfloat16 [16, 2048, 6144], P('grp', None, 'dp'), may hold values from -6 to 6
Outputs:
- mixed_gate: bfloat16 [16, 2048, 6144], P('grp', None, 'dp')
- mixed_up: bfloat16 [16, 2048, 6144], P('grp', None, 'dp')
All inputs are finite; a program needn't handle non-finite values.
Results may differ from a plain program's by a relative error of at most 0.0052.
Values may be sent and summed in bfloat16 or wider, within the bound.
A program may use at most 256 MiB of HBM per device.

v0:
```python
import jax
import jax.numpy as jnp
from jax import lax
from jax.sharding import PartitionSpec as P


def from_behind(x, axis, by):
    size = lax.axis_size(axis)
    return lax.ppermute(x, axis, [(i, (i + by) % size) for i in range(size)])


def gating(rows, cotangent, gate_weight, up_weight):
    scale = rows.shape[1] ** (-0.5)
    gate = jnp.dot(rows, gate_weight, preferred_element_type=jnp.float32) * scale
    up = jnp.dot(rows, up_weight, preferred_element_type=jnp.float32) * scale
    sigma = jax.nn.sigmoid(gate)
    upstream = cotangent.astype(jnp.float32)
    gate_rows = upstream * up * sigma * (1.0 + gate * (1.0 - sigma))
    up_rows = upstream * gate * sigma
    return jnp.stack([gate_rows, up_rows]).astype(jnp.bfloat16)


def local(tokens, hidden_grad, w_gate, w_up):
    local_rows = tokens[0]
    gate_weight = w_gate[0]
    up_weight = w_up[0]
    width = local_rows.shape[1]
    scale = width ** (-0.5)
    unit_cotangent = lax.all_to_all(hidden_grad[0], "dp", split_axis=1, concat_axis=0, tiled=True)
    gathered = lax.all_gather(local_rows, "dp", axis=0, tiled=True)
    unit_rows = gating(gathered, unit_cotangent, gate_weight, up_weight)
    gradient = jnp.einsum("rd,krf->kdf", gathered, unit_rows, preferred_element_type=jnp.float32)
    weights = jnp.concatenate([w_gate, w_up], axis=0).astype(jnp.float32)
    stepped = (weights - 0.5 * (gradient * scale)).astype(jnp.bfloat16)
    left_side = from_behind(stepped, "grp", 1)
    right_side = from_behind(stepped, "grp", -1)
    mixed = 0.5 * stepped.astype(jnp.float32) + 0.25 * (
        left_side.astype(jnp.float32) + right_side.astype(jnp.float32)
    )
    mixed = mixed.astype(jnp.bfloat16)
    return (mixed[0:1], mixed[1:2])


def solution(mesh):
    in_specs = (
        P("grp", "dp", None),
        P("grp", "dp", None),
        P("grp", None, "dp"),
        P("grp", None, "dp"),
    )
    out_specs = (P("grp", None, "dp"), P("grp", None, "dp"))
    return jax.shard_map(local, mesh=mesh, in_specs=in_specs, out_specs=out_specs, check_vma=False)
```

profile of v0, /device:TPU:32, one launch (start us, length us, event | category | flops | bytes accessed | tf_op | source)
XLA Modules:
  0.0 318.6 jit_solution(314343980765271977)
XLA Ops:
  7.2 0.0 all-gather.3.cloned.1.call-start
  7.2 0.7 all-gather.3.cloned.1.call-update
  7.9 1.7 copy.13
  9.6 0.0 copy-start
  9.6 1.5 copy.8
  11.1 0.0 copy-start.1
  11.1 8.6 %all-to-all-start = ((bf16[128,16,384]{2,0,1:T(8,128)(2,1)}), bf16[128,16,384]{2,0,1:T(8,128)(2,1)}, u32[]{:S(2)}, u32[]{:S(2)}) async-start(bf16[128,16,384]{2,0,1:T(8,128)(2,1)} %copy.8), calls=%async_computation | async-start | bytes 3145728 | tf_op jit(solution)/shard_map/all_to_all | solution.py:29
  19.8 0.0 copy-done
  19.8 1.6 copy.6
  21.4 0.0 copy-done.1
  21.4 1.6 copy.7
  23.0 117.8 %all-to-all-done = bf16[128,16,384]{2,0,1:T(8,128)(2,1)} async-done(((bf16[128,16,384]{2,0,1:T(8,128)(2,1)}), bf16[128,16,384]{2,0,1:T(8,128)(2,1)}, u32[]{:S(2)}, u32[]{:S(2)}) %all-to-all-start) | async-done | bytes 1572896 | tf_op jit(solution)/shard_map/all_to_all | solution.py:29
  140.8 0.0 all-gather.3.cloned.1.call-done
  140.8 0.0 copy-start.4
  140.8 9.3 %fusion.16 = (bf16[2048,384]{1,0:T(8,128)(2,1)S(1)}, f32[2048,384]{1,0:T(8,128)S(1)}) fusion(bf16[128,16,384]{2,0,1:T(8,128)(2,1)} %all-to-all-done, bf16[1,2048,384]{2,1,0:T(8,128)(2,1)S(1)} %copy-done, bf16[1,2048,2048]{2,1,0:T(8,128)(2,1)} %all-gather.3.cloned.1.call-done), kind=kOutput, calls=%fused_computation.18 | convolution fusion | flops 3227516928 | bytes 16252928 | tf_op jit(solution)/shard_map/dot_general | solution.py:14
  150.1 0.0 copy-done.4
  150.1 0.0 copy-start.2
  150.1 0.0 copy-start.3
  150.1 6.7 %fusion.22 = bf16[1,2048,384]{2,1,0:T(8,128)(2,1)S(1)} fusion(f32[2048,384]{1,0:T(8,128)S(1)} %get-tuple-element.7, bf16[1,2048,2048]{2,1,0:T(8,128)(2,1)S(1)} %copy-done.4, bf16[128,16,384]{2,0,1:T(8,128)(2,1)} %all-to-all-done, bf16[1,2048,384]{2,1,0:T(8,128)(2,1)S(1)} %copy-done.1), kind=kOutput, calls=%fused_computation.21 | convolution fusion | flops 3230662656 | bytes 16252928 | tf_op jit(solution)/shard_map/dot_general | solution.py:15
  156.8 0.0 copy-done.2
  156.8 0.0 copy-done.3
  156.8 8.8 %fusion.6 = bf16[2,2048,384]{1,2,0:T(8,128)(2,1)S(1)} fusion(bf16[1,2048,2048]{2,1,0:T(8,128)(2,1)S(1)} %copy-done.4, bf16[1,2048,384]{1,2,0:T(8,128)(2,1)S(1)} %copy-done.3, bf16[1,2048,384]{1,2,0:T(8,128)(2,1)S(1)} %copy-done.2, bf16[1,2048,384]{2,1,0:T(8,128)(2,1)S(1)} %bitcast.55, bf16[1,2048,384]{2,1,0:T(8,128)(2,1)S(1)} %fusion.22), kind=kOutput, calls=%fused_computation.7 | convolution fusion | flops 6451888128 | bytes 17825792 | tf_op jit(solution)/shard_map/rd,krf->kdf/dot_general | solution.py:32
  165.6 0.1 collective-permute-start
  165.7 7.8 %collective-permute-start.1 = (bf16[2,2048,384]{1,2,0:T(8,128)(2,1)S(1)}, bf16[2,2048,384]{1,2,0:T(8,128)(2,1)S(1)}, u32[]{:S(2)}, u32[]{:S(2)}) collective-permute-start(bf16[2,2048,384]{1,2,0:T(8,128)(2,1)S(1)} %fusion.6), channel_id=1, source_target_pairs={{0,240},{16,0},{32,16},{48,32},{64,48},{80,64},{96,80},{112,96},{1... | collective-permute-start | bytes 9437192 | tf_op jit(solution)/shard_map/ppermute | solution.py:9
  173.4 132.2 %collective-permute-done = bf16[2,2048,384]{1,2,0:T(8,128)(2,1)S(1)} collective-permute-done((bf16[2,2048,384]{1,2,0:T(8,128)(2,1)S(1)}, bf16[2,2048,384]{1,2,0:T(8,128)(2,1)S(1)}, u32[]{:S(2)}, u32[]{:S(2)}) %collective-permute-start) | collective-permute-done | bytes 3145760 | tf_op jit(solution)/shard_map/ppermute | solution.py:9
  305.7 0.0 collective-permute-done.1
  305.7 2.5 add_convert_fusion
  308.2 0.4 fusion.28
  308.6 1.6 copy.10
  310.2 1.6 copy.11
Async XLA Ops:
  7.2 133.6 %all-gather.3.cloned.1.call-start = ((), (), s32[]{:S(2)}) async-start(), calls=%async_computation.1 | async-start | bytes 8912896 | tf_op jit(solution)/shard_map/all_gather | solution.py:30
  9.6 10.1 %copy-start = (bf16[1,2048,384]{2,1,0:T(8,128)(2,1)S(1)}, bf16[1,2048,384]{2,1,0:T(8,128)(2,1)}, u32[]{:S(2)}) copy-start(bf16[1,2048,384]{2,1,0:T(8,128)(2,1)} %param.6) | copy-start | bytes 4718596
  11.1 10.3 %copy-start.1 = (bf16[1,2048,384]{2,1,0:T(8,128)(2,1)S(1)}, bf16[1,2048,384]{2,1,0:T(8,128)(2,1)}, u32[]{:S(2)}) copy-start(bf16[1,2048,384]{2,1,0:T(8,128)(2,1)} %param.7) | copy-start | bytes 4718596
  11.1 129.6 %all-to-all-start = ((bf16[128,16,384]{2,0,1:T(8,128)(2,1)}), bf16[128,16,384]{2,0,1:T(8,128)(2,1)}, u32[]{:S(2)}, u32[]{:S(2)}) async-start(bf16[128,16,384]{2,0,1:T(8,128)(2,1)} %copy.8), calls=%async_computation | async-start | bytes 3145728 | tf_op jit(solution)/shard_map/all_to_all | solution.py:29
  140.8 9.3 %copy-start.4 = (bf16[1,2048,2048]{2,1,0:T(8,128)(2,1)S(1)}, bf16[1,2048,2048]{2,1,0:T(8,128)(2,1)}, u32[]{:S(2)}) copy-start(bf16[1,2048,2048]{2,1,0:T(8,128)(2,1)} %all-gather.3.cloned.1.call-done) | copy-start | bytes 25165828
  150.1 6.7 %copy-start.2 = (bf16[1,2048,384]{1,2,0:T(8,128)(2,1)S(1)}, bf16[1,2048,384]{1,2,0:T(8,128)(2,1)}, u32[]{:S(2)}) copy-start(bf16[1,2048,384]{1,2,0:T(8,128)(2,1)} %copy.6) | copy-start | bytes 4718596
  150.1 6.7 %copy-start.3 = (bf16[1,2048,384]{1,2,0:T(8,128)(2,1)S(1)}, bf16[1,2048,384]{1,2,0:T(8,128)(2,1)}, u32[]{:S(2)}) copy-start(bf16[1,2048,384]{1,2,0:T(8,128)(2,1)} %copy.7) | copy-start | bytes 4718596
  165.6 140.1 %collective-permute-start = (bf16[2,2048,384]{1,2,0:T(8,128)(2,1)S(1)}, bf16[2,2048,384]{1,2,0:T(8,128)(2,1)S(1)}, u32[]{:S(2)}, u32[]{:S(2)}) collective-permute-start(bf16[2,2048,384]{1,2,0:T(8,128)(2,1)S(1)} %fusion.6), channel_id=1, source_target_pairs={{0,16},{16,32},{32,48},{48,64},{64,80},{80,96},{96,112},{112,128},... | collective-permute-start | bytes 9437192 | tf_op jit(solution)/shard_map/ppermute | solution.py:9
  165.7 140.0 %collective-permute-start.1 = (bf16[2,2048,384]{1,2,0:T(8,128)(2,1)S(1)}, bf16[2,2048,384]{1,2,0:T(8,128)(2,1)S(1)}, u32[]{:S(2)}, u32[]{:S(2)}) collective-permute-start(bf16[2,2048,384]{1,2,0:T(8,128)(2,1)S(1)} %fusion.6), channel_id=1, source_target_pairs={{0,240},{16,0},{32,16},{48,32},{64,48},{80,64},{96,80},{112,96},{1... | collective-permute-start | bytes 9437192 | tf_op jit(solution)/shard_map/ppermute | solution.py:9
Sparse Core Ops, SparseCore 0:
  9.8 126.8 all-gather.2
where the time goes:
time: 322 us; the launch traced here: 319 us
  waiting for transfers between devices  251 us (78%)
  matrix products  24.7 us (8%)
  starting transfers between devices  16.5 us (5%)
  between operations  14.1 us (4%)
  local copies, waits for them, and re-layouts  10 us (3%)
    ppermute x2, waiting for transfers between devices, from_behind(): return lax.ppermute(x, axis, [(i, (i + by) % size) for i in range(size)])  132 us
    all_to_all x1, waiting for transfers between devices, local(): lax.all_to_all(hidden_grad[0], 'dp', split_axis=1, concat_axis=0, tiled=T...  118 us
    dot_general x1, matrix products, gating(): jnp.dot(rows, gate_weight, preferred_element_type=jnp.float32) * scale  9.29 us
    dot_general x1, matrix products, local(): jnp.einsum('rd,krf->kdf', gathered, unit_rows, preferred_element_type=jnp...  8.78 us
    all_to_all x1, starting transfers between devices, local(): lax.all_to_all(hidden_grad[0], 'dp', split_axis=1, concat_axis=0, tiled=T...  8.61 us
    unnamed x15, local copies, waits for them, and re-layouts  8.12 us
    ppermute x2, starting transfers between devices, from_behind(): return lax.ppermute(x, axis, [(i, (i + by) % size) for i in range(size)])  7.83 us
    dot_general x1, matrix products, gating(): up = jnp.dot(rows, up_weight, preferred_element_type=jnp.float32) * scale  6.67 us
  transfers between devices with their start and end apart: 4, of which 2 were waited for; matrix products, arithmetic and copies ran while one was open for 2% of the time, Pallas kernels for 0%

commit v1 on v0

v1 whole, which is shorter than its diff:
```python
import functools

import jax
import jax.numpy as jnp
from jax import lax
from jax.experimental import pallas as pl
from jax.experimental.pallas import tpu as pltpu
from jax.sharding import PartitionSpec as P

MESH = pl.DeviceIdType.MESH
LINE = 4
STAGGER = True


def kernel(
    groups, tokens, hidden_grad, w_gate, w_up, out_gate, out_up,
    tok, cot, wts, rows, acc, grad, step, from_twin, from_far,
    load_sem, own_sem,
    z_send, z_recv, x_send, x_recv, half_send, half_recv,
    cot_send, cot_recv, step_send, step_recv, out_sem, turn,
):
    width = tok.shape[1]
    scale = width ** (-0.5)
    shard = tokens.shape[1]
    units = w_gate.shape[2]
    chunk = LINE * shard
    tall = 256
    blocks = width // tall

    g = lax.axis_index("grp")
    d = lax.axis_index("dp")
    z, x = d // LINE, d % LINE
    core = g % 2
    even = core == 0
    odd = core == 1
    twin = g + 1 - 2 * core
    far = (g - 1 + 2 * core + groups) % groups
    x_left, x_right, x_opp = (x + 3) % LINE, (x + 1) % LINE, (x + 2) % LINE

    def row_of(k):
        flip = z // 2
        low = z + flip * (3 - 2 * z)
        near = (1 - k // 2) * ((low + k) % 2) + (k // 2) * k
        return near + flip * (3 - 2 * near)

    barrier = pltpu.get_barrier_semaphore()

    def greet(i, carry):
        peer = (d + i) % 16
        pl.semaphore_signal(barrier, inc=1, device_id=(g, peer), device_id_type=MESH)
        return carry

    lax.fori_loop(1, 16, greet, 0)
    pl.semaphore_signal(barrier, inc=1, device_id=(twin, d), device_id_type=MESH)
    pl.semaphore_signal(barrier, inc=1, device_id=(far, d), device_id_type=MESH)

    def shard_at(row, col):
        return pl.ds(pl.multiple_of((row * LINE + col) * shard, shard), shard)

    loads = [
        pltpu.make_async_copy(tokens.at[0], tok.at[shard_at(z, x)], own_sem),
        pltpu.make_async_copy(w_gate.at[0], wts.at[:, pl.ds(0, units)], load_sem.at[0]),
        pltpu.make_async_copy(w_up.at[0], wts.at[:, pl.ds(units, units)], load_sem.at[1]),
        pltpu.make_async_copy(
            hidden_grad.at[0, :, pl.ds(pl.multiple_of(d * units, 128), units)],
            cot.at[shard_at(z, x)],
            load_sem.at[2],
        ),
    ]
    for load in loads:
        load.start()
    grad[...] = jnp.zeros_like(grad)
    loads[0].wait()
    pl.semaphore_wait(barrier, 17)

    def z_copy(row, way, to):
        return pltpu.make_async_remote_copy(
            src_ref=tok.at[shard_at(row, x)],
            dst_ref=tok.at[shard_at(row, x)],
            send_sem=z_send.at[way, row],
            recv_sem=z_recv.at[row],
            device_id=(g, to * LINE + x),
            device_id_type=MESH,
        )

    def x_copy(row, col, way):
        to = x_right if way == 0 else x_left
        return pltpu.make_async_remote_copy(
            src_ref=tok.at[shard_at(row, col)],
            dst_ref=tok.at[shard_at(row, col)],
            send_sem=x_send.at[way, row],
            recv_sem=x_recv.at[way, row],
            device_id=(g, z * LINE + to),
            device_id_type=MESH,
        )

    def half_copy(row, col, way):
        half = shard // 2
        at = pl.ds(pl.multiple_of((row * LINE + col) * shard + way * half, half), half)
        to = x_right if way == 0 else x_left
        return pltpu.make_async_remote_copy(
            src_ref=tok.at[at],
            dst_ref=tok.at[at],
            send_sem=half_send.at[way, row],
            recv_sem=half_recv.at[way, row],
            device_id=(g, z * LINE + to),
            device_id_type=MESH,
        )

    def send_z(row):
        @pl.when((z < LINE - 1) & (row <= z))
        def _():
            z_copy(row, 0, z + 1).start()

        @pl.when((z > 0) & (row >= z))
        def _():
            z_copy(row, 1, z - 1).start()

    def take_z(row):
        z_copy(row, 0, z).wait_recv()
        send_z(row)

    def send_x(row):
        x_copy(row, x, 0).start()
        x_copy(row, x, 1).start()

    def relay_x(row):
        x_copy(row, x_left, 0).wait_recv()
        half_copy(row, x_left, 0).start()
        x_copy(row, x_right, 1).wait_recv()
        half_copy(row, x_right, 1).start()

    def cot_copy(i):
        peer = (d + i) % 16
        return pltpu.make_async_remote_copy(
            src_ref=hidden_grad.at[0, :, pl.ds(pl.multiple_of(peer * units, 128), units)],
            dst_ref=cot.at[shard_at(z, x)],
            send_sem=cot_send.at[i],
            recv_sem=cot_recv.at[d],
            device_id=(g, peer),
            device_id_type=MESH,
        )

    def take_cot(source):
        pltpu.make_async_remote_copy(
            src_ref=cot.at[pl.ds(pl.multiple_of(source * shard, shard), shard)],
            dst_ref=cot.at[pl.ds(pl.multiple_of(source * shard, shard), shard)],
            send_sem=cot_send.at[0],
            recv_sem=cot_recv.at[source],
            device_id=(g, source),
            device_id_type=MESH,
        ).wait_recv()

    def gating(row):
        for col in (x_left, x_right, x_opp):
            take_cot(row * LINE + col)

        @pl.when(row != z)
        def _():
            take_cot(row * LINE + x)

        def part(m, carry):
            at = pl.ds(pl.multiple_of(row * chunk + m * tall, tall), tall)
            acc[...] = jnp.dot(tok[at, :], wts[...], preferred_element_type=jnp.float32)
            gate = acc[:, :units] * scale
            up = acc[:, units:] * scale
            sigma = jax.nn.sigmoid(gate)
            upstream = cot[at, :].astype(jnp.float32)
            to = pl.ds(pl.multiple_of(m * tall, tall), tall)
            rows[to, :units] = (upstream * up * sigma * (1.0 + gate * (1.0 - sigma))).astype(jnp.bfloat16)
            rows[to, units:] = (upstream * gate * sigma).astype(jnp.bfloat16)
            return carry

        lax.fori_loop(0, chunk // tall, part, 0)

    def gradient(row, b):
        at = pl.ds(pl.multiple_of(row * chunk, chunk), chunk)
        to = pl.ds(pl.multiple_of(b * tall, tall), tall)
        return grad[to, :] + lax.dot_general(
            tok[at, to], rows[...], (((0,), (0,)), ((), ())), preferred_element_type=jnp.float32
        )

    def finish_row(row):
        half_copy(row, x_opp, 0).wait_recv()
        half_copy(row, x_opp, 1).wait_recv()
        gating(row)

    def middle(row):
        finish_row(row)

        def block(b, carry):
            to = pl.ds(pl.multiple_of(b * tall, tall), tall)
            grad[to, :] = gradient(row, b)
            return carry

        lax.fori_loop(0, blocks, block, 0)

    if STAGGER:
        @pl.when(odd)
        def _():
            pl.semaphore_wait(turn.at[0], 1)

    send_z(z)
    if STAGGER:
        @pl.when(even)
        def _():
            send_x(z)
    else:
        send_x(z)

    def exchange(i, carry):
        cot_copy(i).start()
        return carry

    lax.fori_loop(1, 16, exchange, 0)
    for load in loads[1:]:
        load.wait()

    def my_turn(i):
        pl.semaphore_signal(turn.at[i], inc=1, device_id=(twin, d), device_id_type=MESH)

    if STAGGER:
        @pl.when(odd)
        def _():
            for k in range(1, LINE):
                take_z(row_of(k))
            pl.semaphore_wait(turn.at[1], 1)
            send_x(z)

    def stage(k, carry):
        @pl.when(k < LINE - 1)
        def _():
            row = row_of(k + 1)
            if STAGGER:
                @pl.when(even)
                def _():
                    take_z(row)
            else:
                take_z(row)
            send_x(row)

        if STAGGER:
            @pl.when(even & (k == 2))
            def _():
                my_turn(0)

        relay_x(row_of(k))

        if STAGGER:
            @pl.when(even & (k == 3))
            def _():
                my_turn(1)

        @pl.when(k > 0)
        def _():
            middle(row_of(k - 1))

        return carry

    lax.fori_loop(0, LINE, stage, 0)

    last = row_of(LINE - 1)
    finish_row(last)

    def step_copy(b, way):
        to = pl.ds(pl.multiple_of(b * tall, tall), tall)
        return pltpu.make_async_remote_copy(
            src_ref=step.at[to],
            dst_ref=(from_twin if way == 0 else from_far).at[to],
            send_sem=step_send.at[way, b],
            recv_sem=step_recv.at[way, b],
            device_id=((twin if way == 0 else far), d),
            device_id_type=MESH,
        )

    def send_step(b):
        step_copy(b, 1).start()
        step_copy(b, 0).start()

    def final(b, carry):
        to = pl.ds(pl.multiple_of(b * tall, tall), tall)
        moved = wts[to, :].astype(jnp.float32) - 0.5 * (gradient(last, b) * scale)
        step[to, :] = moved.astype(jnp.bfloat16)

        @pl.when(b > 0)
        def _():
            send_step(b - 1)

        return carry

    lax.fori_loop(0, blocks, final, 0)
    send_step(blocks - 1)

    def out_copies(b):
        to = pl.ds(pl.multiple_of(b * tall, tall), tall)
        return (
            pltpu.make_async_copy(from_far.at[to, pl.ds(0, units)], out_gate.at[0, to], out_sem.at[0, b]),
            pltpu.make_async_copy(from_far.at[to, pl.ds(units, units)], out_up.at[0, to], out_sem.at[1, b]),
        )

    def mix(b, carry):
        to = pl.ds(pl.multiple_of(b * tall, tall), tall)
        step_copy(b, 0).wait_recv()
        step_copy(b, 1).wait_recv()
        mixed = 0.5 * step[to, :].astype(jnp.float32) + 0.25 * (
            from_twin[to, :].astype(jnp.float32) + from_far[to, :].astype(jnp.float32)
        )
        from_far[to, :] = mixed.astype(jnp.bfloat16)
        for copy in out_copies(b):
            copy.start()
        return carry

    lax.fori_loop(0, blocks, mix, 0)

    def sent_rows(k, carry):
        row = row_of(k)
        @pl.when((z < LINE - 1) & (row <= z))
        def _():
            z_copy(row, 0, z + 1).wait_send()

        @pl.when((z > 0) & (row >= z))
        def _():
            z_copy(row, 1, z - 1).wait_send()

        x_copy(row, x, 0).wait_send()
        x_copy(row, x, 1).wait_send()
        half_copy(row, x_left, 0).wait_send()
        half_copy(row, x_right, 1).wait_send()
        return carry

    lax.fori_loop(0, LINE, sent_rows, 0)

    def sent_cot(i, carry):
        cot_copy(i).wait_send()
        return carry

    lax.fori_loop(1, 16, sent_cot, 0)

    def sent_blocks(b, carry):
        step_copy(b, 0).wait_send()
        step_copy(b, 1).wait_send()
        for copy in out_copies(b):
            copy.wait()
        return carry

    lax.fori_loop(0, blocks, sent_blocks, 0)


def solution(mesh):
    groups = mesh.shape["grp"]

    def local(tokens, hidden_grad, w_gate, w_up):
        shard, width = tokens.shape[1:]
        units = w_gate.shape[2]
        count = shard * mesh.shape["dp"]
        chunk = LINE * shard
        tall = 256
        blocks = width // tall
        dma = pltpu.SemaphoreType.DMA
        out = jax.ShapeDtypeStruct(w_gate.shape, jnp.bfloat16)
        wide = 2 * units
        return pl.pallas_call(
            functools.partial(kernel, groups),
            out_shape=(out, out),
            in_specs=[pl.BlockSpec(memory_space=pl.ANY)] * 4,
            out_specs=(pl.BlockSpec(memory_space=pl.ANY),) * 2,
            scratch_shapes=[
                pltpu.VMEM((count, width), jnp.bfloat16),
                pltpu.VMEM((count, units), jnp.bfloat16),
                pltpu.VMEM((width, wide), jnp.bfloat16),
                pltpu.VMEM((chunk, wide), jnp.bfloat16),
                pltpu.VMEM((tall, wide), jnp.float32),
                pltpu.VMEM((width, wide), jnp.float32),
                pltpu.VMEM((width, wide), jnp.bfloat16),
                pltpu.VMEM((width, wide), jnp.bfloat16),
                pltpu.VMEM((width, wide), jnp.bfloat16),
                dma((3,)),
                dma(()),
                dma((2, LINE)),
                dma((LINE,)),
                dma((2, LINE)),
                dma((2, LINE)),
                dma((2, LINE)),
                dma((2, LINE)),
                dma((16,)),
                dma((16,)),
                dma((2, blocks)),
                dma((2, blocks)),
                dma((2, blocks)),
                pltpu.SemaphoreType.REGULAR((2,)),
            ],
            compiler_params=pltpu.CompilerParams(
                collective_id=0, has_side_effects=True, vmem_limit_bytes=60 * 1024 * 1024
            ),
        )(tokens, hidden_grad, w_gate, w_up)

    in_specs = (
        P("grp", "dp", None),
        P("grp", "dp", None),
        P("grp", None, "dp"),
        P("grp", None, "dp"),
    )
    out_specs = (P("grp", None, "dp"), P("grp", None, "dp"))
    return jax.shard_map(local, mesh=mesh, in_specs=in_specs, out_specs=out_specs, check_vma=False)
```

time: 322 us -> 272 us (0.84)
  the two profiles are of different devices: /device:TPU:32 before, /device:TPU:8 now
where the time goes in v1:
time: 272 us
  Pallas kernels  267 us (98%)
  local copies, waits for them, and re-layouts  3.97 us (1%)
    pallas_call x1, Pallas kernels, local(): pl.pallas_call(functools.partial(kernel, groups), out_shape=(out, out), i...  267 us

profile of v1, /device:TPU:8, one launch (start us, length us, event | category | flops | bytes accessed | tf_op | source)
XLA Modules:
  0.0 271.8 jit_solution(1875414376895993404)
XLA Ops:
  0.6 267.2 %shard_map.59 = (bf16[1,2048,384]{2,1,0:T(8,128)(2,1)}, bf16[1,2048,384]{2,1,0:T(8,128)(2,1)}) custom-call(bf16[1,128,2048]{2,1,0:T(8,128)(2,1)} %tokens.1, bf16[1,128,6144]{2,1,0:T(8,128)(2,1)} %hidden_grad.1, bf16[1,2048,384]{2,1,0:T(8,128)(2,1)} %w_gate.1, bf16[1,2048,384]{2,1,0:T(8,128)(2,1)} %w_up.1), custom_call_target="tpu_custom_call" | custom-call | tf_op jit(solution)/shard_map/pallas_call | solution.py:362
  267.8 0.0 copy-start
  267.8 2.8 %copy.8 = bf16[1,2048,384]{2,1,0:T(8,128)(2,1)} copy(bf16[1,2048,384]{2,1,0:T(8,128)(2,1)} %get-tuple-element.4) | data formatting | bytes 3145728
  270.6 0.0 copy-done
  270.6 1.1 copy.9
Async XLA Ops:
  267.8 2.8 %copy-start = (bf16[1,2048,384]{2,1,0:T(8,128)(2,1)S(1)}, bf16[1,2048,384]{2,1,0:T(8,128)(2,1)}, u32[]{:S(2)}) copy-start(bf16[1,2048,384]{2,1,0:T(8,128)(2,1)} %get-tuple-element.5) | copy-start | bytes 4718596

commit v2 on v1

v2 whole, which is shorter than its diff:
```python
import functools

import jax
import jax.numpy as jnp
from jax import lax
from jax.experimental import pallas as pl
from jax.experimental.pallas import tpu as pltpu
from jax.sharding import PartitionSpec as P

MESH = pl.DeviceIdType.MESH
LINE = 4
PIECES = 2
TURN_Z = 2
INNER_AT = 1
OUTER_AT = 2
EARLY_ROWS = 1
OUTER_ODD = 0


def kernel(
    groups, tokens, hidden_grad, w_gate, w_up, out,
    tok, cot, wts, rows, acc, step, from_twin, from_far,
    load_sem, own_sem,
    z_send, z_recv, x_send, x_recv, half_send, half_recv,
    cot_send, cot_recv, step_send, step_recv, out_sem, turn,
):
    width = tok.shape[1]
    scale = width ** (-0.5)
    shard = tokens.shape[1]
    units = w_gate.shape[2]
    chunk = LINE * shard
    tall = 256
    blocks = width // tall

    g = lax.axis_index("grp")
    d = lax.axis_index("dp")
    z, x = d // LINE, d % LINE
    core = g % 2
    even = core == 0
    odd = core == 1
    twin = g + 1 - 2 * core
    far = (g - 1 + 2 * core + groups) % groups
    x_left, x_right, x_opp = (x + 3) % LINE, (x + 1) % LINE, (x + 2) % LINE

    def row_of(k):
        flip = z // 2
        low = z + flip * (3 - 2 * z)
        near = (1 - k // 2) * ((low + k) % 2) + (k // 2) * k
        return near + flip * (3 - 2 * near)

    barrier = pltpu.get_barrier_semaphore()

    def greet(i, carry):
        peer = (d + i) % 16
        pl.semaphore_signal(barrier, inc=1, device_id=(g, peer), device_id_type=MESH)
        return carry

    lax.fori_loop(1, 16, greet, 0)
    pl.semaphore_signal(barrier, inc=1, device_id=(twin, d), device_id_type=MESH)
    pl.semaphore_signal(barrier, inc=1, device_id=(far, d), device_id_type=MESH)

    def shard_at(row, col):
        return pl.ds(pl.multiple_of((row * LINE + col) * shard, shard), shard)

    loads = [
        pltpu.make_async_copy(tokens.at[0], tok.at[shard_at(z, x)], own_sem),
        pltpu.make_async_copy(w_gate.at[0], wts.at[:, pl.ds(0, units)], load_sem.at[0]),
        pltpu.make_async_copy(w_up.at[0], wts.at[:, pl.ds(units, units)], load_sem.at[1]),
        pltpu.make_async_copy(
            hidden_grad.at[0, :, pl.ds(pl.multiple_of(d * units, 128), units)],
            cot.at[shard_at(z, x)],
            load_sem.at[2],
        ),
    ]
    for load in loads:
        load.start()
    def meet():
        loads[0].wait()
        pl.semaphore_wait(barrier, 17)

    meet()

    part_rows = shard // PIECES

    def piece_at(row, col, p):
        return pl.ds(pl.multiple_of((row * LINE + col) * shard + p * part_rows, part_rows), part_rows)

    def z_copy(row, p, way, to):
        return pltpu.make_async_remote_copy(
            src_ref=tok.at[piece_at(row, x, p)],
            dst_ref=tok.at[piece_at(row, x, p)],
            send_sem=z_send.at[way, row, p],
            recv_sem=z_recv.at[row, p],
            device_id=(g, to * LINE + x),
            device_id_type=MESH,
        )

    def x_copy(row, col, p, way):
        to = x_right if way == 0 else x_left
        return pltpu.make_async_remote_copy(
            src_ref=tok.at[piece_at(row, col, p)],
            dst_ref=tok.at[piece_at(row, col, p)],
            send_sem=x_send.at[way, row, p],
            recv_sem=x_recv.at[way, row, p],
            device_id=(g, z * LINE + to),
            device_id_type=MESH,
        )

    def far_copy(row, col, way):
        to = x_right if way == 0 else x_left
        return pltpu.make_async_remote_copy(
            src_ref=tok.at[piece_at(row, col, way)],
            dst_ref=tok.at[piece_at(row, col, way)],
            send_sem=half_send.at[way, row],
            recv_sem=half_recv.at[way, row],
            device_id=(g, z * LINE + to),
            device_id_type=MESH,
        )

    def send_z(row, p):
        @pl.when((z < LINE - 1) & (row <= z))
        def _():
            z_copy(row, p, 0, z + 1).start()

        @pl.when((z > 0) & (row >= z))
        def _():
            z_copy(row, p, 1, z - 1).start()

    def take_z(row, p):
        z_copy(row, p, 0, z).wait_recv()
        send_z(row, p)

    def send_x(row, p):
        x_copy(row, x, p, 0).start()
        x_copy(row, x, p, 1).start()

    def relay_x(row):
        x_copy(row, x_left, 0, 0).wait_recv()
        far_copy(row, x_left, 0).start()
        x_copy(row, x_right, 1, 1).wait_recv()
        far_copy(row, x_right, 1).start()

    def cot_copy(peer):
        return pltpu.make_async_remote_copy(
            src_ref=hidden_grad.at[0, :, pl.ds(pl.multiple_of(peer * units, 128), units)],
            dst_ref=cot.at[shard_at(z, x)],
            send_sem=cot_send.at[peer],
            recv_sem=cot_recv.at[d],
            device_id=(g, peer),
            device_id_type=MESH,
        )

    def exchange(row):
        def one(i, carry):
            cot_copy(row * LINE + (x + 4 - i) % LINE).start()
            return carry

        lax.fori_loop(1, LINE, one, 0)

        @pl.when(row != z)
        def _():
            cot_copy(row * LINE + x).start()

    def exchange_inner():
        exchange(z)
        for row in range(1, LINE - 1):
            @pl.when(row != z)
            def _():
                exchange(row)

    def exchange_outer():
        for row in (0, LINE - 1):
            @pl.when(row != z)
            def _():
                exchange(row)

    def take_cot(source):
        pltpu.make_async_remote_copy(
            src_ref=cot.at[pl.ds(pl.multiple_of(source * shard, shard), shard)],
            dst_ref=cot.at[pl.ds(pl.multiple_of(source * shard, shard), shard)],
            send_sem=cot_send.at[0],
            recv_sem=cot_recv.at[source],
            device_id=(g, source),
            device_id_type=MESH,
        ).wait_recv()

    def gating(row):
        for col in (x_left, x_right, x_opp):
            take_cot(row * LINE + col)

        @pl.when(row != z)
        def _():
            take_cot(row * LINE + x)

        def part(m, carry):
            at = pl.ds(pl.multiple_of(row * chunk + m * tall, tall), tall)
            acc[...] = jnp.dot(tok[at, :], wts[...], preferred_element_type=jnp.float32)
            gate = acc[:, :units] * scale
            up = acc[:, units:] * scale
            sigma = jax.nn.sigmoid(gate)
            upstream = cot[at, :].astype(jnp.float32)
            rows[at, :units] = (upstream * up * sigma * (1.0 + gate * (1.0 - sigma))).astype(jnp.bfloat16)
            rows[at, units:] = (upstream * gate * sigma).astype(jnp.bfloat16)
            return carry

        lax.fori_loop(0, chunk // tall, part, 0)

    def gradient(b):
        to = pl.ds(pl.multiple_of(b * tall, tall), tall)
        return lax.dot_general(
            tok[:, to], rows[...], (((0,), (0,)), ((), ())), preferred_element_type=jnp.float32
        )

    def finish_row(row):
        x_copy(row, x_left, 1, 0).wait_recv()
        x_copy(row, x_right, 0, 1).wait_recv()
        far_copy(row, x_opp, 0).wait_recv()
        far_copy(row, x_opp, 1).wait_recv()
        gating(row)

    def my_turn(i):
        pl.semaphore_signal(turn.at[i], inc=1, device_id=(twin, d), device_id_type=MESH)

    def wait_turn(i):
        pl.semaphore_wait(turn.at[i], 1)

    @pl.when(odd)
    def _():
        if OUTER_ODD == 0:
            exchange_outer()
        if TURN_Z >= 0:
            wait_turn(0)

    for p in range(PIECES):
        send_z(z, p)

    @pl.when(even)
    def _():
        for p in range(PIECES):
            send_x(z, p)

    @pl.when(even)
    def _():
        if TURN_Z == 0:
            my_turn(0)

    if INNER_AT == 0:
        exchange_inner()

    for k in range(1, LINE):
        row = row_of(k)
        for p in range(PIECES):
            take_z(row, p)

            @pl.when(even)
            def _():
                send_x(row, p)

        @pl.when(even)
        def _():
            if k == TURN_Z:
                my_turn(0)
            relay_x(row_of(k - 1))

        if k == INNER_AT:
            exchange_inner()
        if k == OUTER_AT and k == OUTER_ODD:
            exchange_outer()
        elif k == OUTER_AT:
            pl.when(even)(exchange_outer)
        elif k == OUTER_ODD:
            pl.when(odd)(exchange_outer)

    for load in loads[1:]:
        load.wait()

    @pl.when(odd)
    def _():
        wait_turn(1)
        for k in range(LINE):
            for p in range(PIECES):
                send_x(row_of(k), p)
        for k in range(LINE - 1):
            relay_x(row_of(k))

    def all_rows(k, carry):
        finish_row(row_of(k))
        return carry

    lax.fori_loop(0, EARLY_ROWS, all_rows, 0)
    relay_x(row_of(LINE - 1))

    @pl.when(even)
    def _():
        my_turn(1)

    lax.fori_loop(EARLY_ROWS, LINE, all_rows, 0)

    def step_copy(b, way):
        to = pl.ds(pl.multiple_of(b * tall, tall), tall)
        return pltpu.make_async_remote_copy(
            src_ref=step.at[to],
            dst_ref=(from_twin if way == 0 else from_far).at[to],
            send_sem=step_send.at[way, b],
            recv_sem=step_recv.at[way, b],
            device_id=((twin if way == 0 else far), d),
            device_id_type=MESH,
        )

    def send_step(b):
        step_copy(b, 1).start()
        step_copy(b, 0).start()

    def final(b, carry):
        to = pl.ds(pl.multiple_of(b * tall, tall), tall)
        moved = wts[to, :].astype(jnp.float32) - 0.5 * (gradient(b) * scale)
        step[to, :] = moved.astype(jnp.bfloat16)

        @pl.when(b > 0)
        def _():
            send_step(b - 1)

        return carry

    lax.fori_loop(0, blocks, final, 0)
    send_step(blocks - 1)

    def out_copies(b):
        to = pl.ds(pl.multiple_of(b * tall, tall), tall)
        return (pltpu.make_async_copy(from_far.at[to], out.at[0, to], out_sem.at[b]),)

    def mix(b, carry):
        to = pl.ds(pl.multiple_of(b * tall, tall), tall)
        step_copy(b, 0).wait_recv()
        step_copy(b, 1).wait_recv()
        mixed = 0.5 * step[to, :].astype(jnp.float32) + 0.25 * (
            from_twin[to, :].astype(jnp.float32) + from_far[to, :].astype(jnp.float32)
        )
        from_far[to, :] = mixed.astype(jnp.bfloat16)
        for copy in out_copies(b):
            copy.start()
        return carry

    lax.fori_loop(0, blocks, mix, 0)

    def sent_rows(k, carry):
        row = row_of(k)

        for p in range(PIECES):
            @pl.when((z < LINE - 1) & (row <= z))
            def _():
                z_copy(row, p, 0, z + 1).wait_send()

            @pl.when((z > 0) & (row >= z))
            def _():
                z_copy(row, p, 1, z - 1).wait_send()

            x_copy(row, x, p, 0).wait_send()
            x_copy(row, x, p, 1).wait_send()

        far_copy(row, x_left, 0).wait_send()
        far_copy(row, x_right, 1).wait_send()
        return carry

    lax.fori_loop(0, LINE, sent_rows, 0)

    def sent_cot(i, carry):
        cot_copy((d + i) % 16).wait_send()
        return carry

    lax.fori_loop(1, 16, sent_cot, 0)

    def sent_blocks(b, carry):
        step_copy(b, 0).wait_send()
        step_copy(b, 1).wait_send()
        for copy in out_copies(b):
            copy.wait()
        return carry

    lax.fori_loop(0, blocks, sent_blocks, 0)


def solution(mesh):
    groups = mesh.shape["grp"]

    def local(tokens, hidden_grad, w_gate, w_up):
        shard, width = tokens.shape[1:]
        units = w_gate.shape[2]
        count = shard * mesh.shape["dp"]
        tall = 256
        blocks = width // tall
        dma = pltpu.SemaphoreType.DMA
        wide = 2 * units
        mixed = pl.pallas_call(
            functools.partial(kernel, groups),
            out_shape=jax.ShapeDtypeStruct((1, width, wide), jnp.bfloat16),
            in_specs=[pl.BlockSpec(memory_space=pl.ANY)] * 4,
            out_specs=pl.BlockSpec(memory_space=pl.ANY),
            scratch_shapes=[
                pltpu.VMEM((count, width), jnp.bfloat16),
                pltpu.VMEM((count, units), jnp.bfloat16),
                pltpu.VMEM((width, wide), jnp.bfloat16),
                pltpu.VMEM((count, wide), jnp.bfloat16),
                pltpu.VMEM((tall, wide), jnp.float32),
                pltpu.VMEM((width, wide), jnp.bfloat16),
                pltpu.VMEM((width, wide), jnp.bfloat16),
                pltpu.VMEM((width, wide), jnp.bfloat16),
                dma((3,)),
                dma(()),
                dma((2, LINE, PIECES)),
                dma((LINE, PIECES)),
                dma((2, LINE, PIECES)),
                dma((2, LINE, PIECES)),
                dma((2, LINE)),
                dma((2, LINE)),
                dma((16,)),
                dma((16,)),
                dma((2, blocks)),
                dma((2, blocks)),
                dma((blocks,)),
                pltpu.SemaphoreType.REGULAR((2,)),
            ],
            compiler_params=pltpu.CompilerParams(
                collective_id=0, has_side_effects=True, vmem_limit_bytes=60 * 1024 * 1024
            ),
        )(tokens, hidden_grad, w_gate, w_up)
        return mixed[:, :, :units], mixed[:, :, units:]

    in_specs = (
        P("grp", "dp", None),
        P("grp", "dp", None),
        P("grp", None, "dp"),
        P("grp", None, "dp"),
    )
    out_specs = (P("grp", None, "dp"), P("grp", None, "dp"))
    return jax.shard_map(local, mesh=mesh, in_specs=in_specs, out_specs=out_specs, check_vma=False)
```

time: 272 us -> 218 us (0.80)
  the two profiles are of different devices: /device:TPU:8 before, /device:TPU:32 now
where the time goes in v2:
time: 218 us; the launch traced here: 217 us
  Pallas kernels  213 us (98%)
  local copies, waits for them, and re-layouts  3.86 us (2%)
    pallas_call x1, Pallas kernels, local(): pl.pallas_call(functools.partial(kernel, groups), out_shape=jax.ShapeDtyp...  213 us

profile of v2, /device:TPU:32, one launch (start us, length us, event | category | flops | bytes accessed | tf_op | source)
XLA Modules:
  0.0 217.4 jit_solution(7349288312083464222)
XLA Ops:
  0.6 212.9 %shard_map.59 = bf16[1,2048,768]{2,1,0:T(8,128)(2,1)} custom-call(bf16[1,128,2048]{2,1,0:T(8,128)(2,1)} %tokens.1, bf16[1,128,6144]{2,1,0:T(8,128)(2,1)} %hidden_grad.1, bf16[1,2048,384]{2,1,0:T(8,128)(2,1)} %w_gate.1, bf16[1,2048,384]{2,1,0:T(8,128)(2,1)} %w_up.1), custom_call_target="tpu_custom_call" | custom-call | tf_op jit(solution)/shard_map/pallas_call | solution.py:394
  213.6 3.9 %fusion = (bf16[1,2048,384]{2,1,0:T(8,128)(2,1)}, bf16[1,2048,384]{2,1,0:T(8,128)(2,1)}) fusion(bf16[1,2048,768]{2,1,0:T(8,128)(2,1)} %shard_map.59), kind=kLoop, calls=%fused_computation | loop fusion | bytes 6291456 | tf_op jit(solution)/shard_map/slice | solution.py:427

commit v3 on v2

--- a/solution.py
+++ b/solution.py
@@ -378,6 +378,33 @@
         return carry
 
     lax.fori_loop(0, blocks, sent_blocks, 0)
+
+
+def split(mixed, out_gate, out_up, held, in_sem, out_sem):
+    units = out_gate.shape[2]
+    blocks = in_sem.shape[0]
+    tall = held.shape[0] // blocks
+
+    def take(b):
+        at = pl.ds(b * tall, tall)
+        return pltpu.make_async_copy(mixed.at[0, at], held.at[at], in_sem.at[b])
+
+    def give(b):
+        at = pl.ds(b * tall, tall)
+        return (
+            pltpu.make_async_copy(held.at[at, pl.ds(0, units)], out_gate.at[0, at], out_sem.at[0, b]),
+            pltpu.make_async_copy(held.at[at, pl.ds(units, units)], out_up.at[0, at], out_sem.at[1, b]),
+        )
+
+    for b in range(blocks):
+        take(b).start()
+    for b in range(blocks):
+        take(b).wait()
+        for copy in give(b):
+            copy.start()
+    for b in range(blocks):
+        for copy in give(b):
+            copy.wait()
 
 
 def solution(mesh):
@@ -424,7 +451,15 @@
                 collective_id=0, has_side_effects=True, vmem_limit_bytes=60 * 1024 * 1024
             ),
         )(tokens, hidden_grad, w_gate, w_up)
-        return mixed[:, :, :units], mixed[:, :, units:]
+        out = jax.ShapeDtypeStruct(w_gate.shape, jnp.bfloat16)
+        return pl.pallas_call(
+            split,
+            out_shape=(out, out),
+            in_specs=[pl.BlockSpec(memory_space=pl.ANY)],
+            out_specs=(pl.BlockSpec(memory_space=pl.ANY),) * 2,
+            scratch_shapes=[pltpu.VMEM((width, wide), jnp.bfloat16), dma((blocks,)), dma((2, blocks))],
+            compiler_params=pltpu.CompilerParams(vmem_limit_bytes=60 * 1024 * 1024),
+        )(mixed)
 
     in_specs = (
         P("grp", "dp", None),

time: 218 us -> 217 us (level)
  local copies, waits for them, and re-layouts: 3.86 us -> 0 us
  Pallas kernels: 213 us -> 216 us
    slice x1 -> x0, local copies, waits for them, and re-layouts: 3.86 us -> none  [local(): return (mixed[:, :, :units], mixed[:, :, units:])]
    pallas_call x0 -> x1, Pallas kernels: none -> 2.85 us  [local(): pl.pallas_call(split, out_shape=(out, out), in_specs=[pl.BlockSpec(memory...]
where the time goes in v3:
time: 217 us; the launch traced here: 216 us
  Pallas kernels  216 us (100%)
    pallas_call x1, Pallas kernels, local(): pl.pallas_call(functools.partial(kernel, groups), out_shape=jax.ShapeDtyp...  213 us

profile of v3, /device:TPU:32, one launch (start us, length us, event | category | flops | bytes accessed | tf_op | source)
XLA Modules:
  0.0 216.4 jit_solution(14246723339224965192)
XLA Ops:
  0.6 212.9 %shard_map.59.mixed = bf16[1,2048,768]{2,1,0:T(8,128)(2,1)} custom-call(bf16[1,128,2048]{2,1,0:T(8,128)(2,1)} %tokens.1, bf16[1,128,6144]{2,1,0:T(8,128)(2,1)} %hidden_grad.1, bf16[1,2048,384]{2,1,0:T(8,128)(2,1)} %w_gate.1, bf16[1,2048,384]{2,1,0:T(8,128)(2,1)} %w_up.1), custom_call_target="tpu_custom_call" | custom-call | tf_op jit(solution)/shard_map/pallas_call | solution.py:421
  213.6 2.9 %shard_map.60 = (bf16[1,2048,384]{2,1,0:T(8,128)(2,1)}, bf16[1,2048,384]{2,1,0:T(8,128)(2,1)}) custom-call(bf16[1,2048,768]{2,1,0:T(8,128)(2,1)} %shard_map.59.mixed), custom_call_target="tpu_custom_call" | custom-call | tf_op jit(solution)/shard_map/pallas_call | solution.py:455

commit v4 on v3

--- a/solution.py
+++ b/solution.py
@@ -9,7 +9,7 @@
 
 MESH = pl.DeviceIdType.MESH
 LINE = 4
-PIECES = 2
+PIECES = 4
 TURN_Z = 2
 INNER_AT = 1
 OUTER_AT = 2
@@ -19,7 +19,7 @@
 
 def kernel(
     groups, tokens, hidden_grad, w_gate, w_up, out,
-    tok, cot, wts, rows, acc, step, from_twin, from_far,
+    tok, cot, held, wts, rows, acc, step, from_twin, from_far,
     load_sem, own_sem,
     z_send, z_recv, x_send, x_recv, half_send, half_recv,
     cot_send, cot_recv, step_send, step_recv, out_sem, turn,
@@ -71,11 +71,13 @@
             cot.at[shard_at(z, x)],
             load_sem.at[2],
         ),
+        pltpu.make_async_copy(hidden_grad.at[0], held, load_sem.at[3]),
     ]
-    for load in loads:
+    for load in (loads[0], loads[4], *loads[1:4]):
         load.start()
     def meet():
         loads[0].wait()
+        loads[4].wait()
         pl.semaphore_wait(barrier, 17)
 
     meet()
@@ -106,13 +108,13 @@
             device_id_type=MESH,
         )
 
-    def far_copy(row, col, way):
+    def far_copy(row, col, p, way):
         to = x_right if way == 0 else x_left
         return pltpu.make_async_remote_copy(
-            src_ref=tok.at[piece_at(row, col, way)],
-            dst_ref=tok.at[piece_at(row, col, way)],
-            send_sem=half_send.at[way, row],
-            recv_sem=half_recv.at[way, row],
+            src_ref=tok.at[piece_at(row, col, p)],
+            dst_ref=tok.at[piece_at(row, col, p)],
+            send_sem=half_send.at[way, row, p],
+            recv_sem=half_recv.at[way, row, p],
             device_id=(g, z * LINE + to),
             device_id_type=MESH,
         )
@@ -134,15 +136,19 @@
         x_copy(row, x, p, 0).start()
         x_copy(row, x, p, 1).start()
 
+    near = range(PIECES // 2)
+    back = range(PIECES // 2, PIECES)
+
     def relay_x(row):
-        x_copy(row, x_left, 0, 0).wait_recv()
-        far_copy(row, x_left, 0).start()
-        x_copy(row, x_right, 1, 1).wait_recv()
-        far_copy(row, x_right, 1).start()
+        for p, q in zip(near, back):
+            x_copy(row, x_left, p, 0).wait_recv()
+            far_copy(row, x_left, p, 0).start()
+            x_copy(row, x_right, q, 1).wait_recv()
+            far_copy(row, x_right, q, 1).start()
 
     def cot_copy(peer):
         return pltpu.make_async_remote_copy(
-            src_ref=hidden_grad.at[0, :, pl.ds(pl.multiple_of(peer * units, 128), units)],
+            src_ref=held.at[:, pl.ds(pl.multiple_of(peer * units, 128), units)],
             dst_ref=cot.at[shard_at(z, x)],
             send_sem=cot_send.at[peer],
             recv_sem=cot_recv.at[d],
@@ -212,10 +218,11 @@
         )
 
     def finish_row(row):
-        x_copy(row, x_left, 1, 0).wait_recv()
-        x_copy(row, x_right, 0, 1).wait_recv()
-        far_copy(row, x_opp, 0).wait_recv()
-        far_copy(row, x_opp, 1).wait_recv()
+        for p, q in zip(near, back):
+            x_copy(row, x_left, q, 0).wait_recv()
+            x_copy(row, x_right, p, 1).wait_recv()
+            far_copy(row, x_opp, p, 0).wait_recv()
+            far_copy(row, x_opp, q, 1).wait_recv()
         gating(row)
 
     def my_turn(i):
@@ -271,7 +278,7 @@
         elif k == OUTER_ODD:
             pl.when(odd)(exchange_outer)
 
-    for load in loads[1:]:
+    for load in loads[1:4]:
         load.wait()
 
     @pl.when(odd)
@@ -325,6 +332,35 @@
     lax.fori_loop(0, blocks, final, 0)
     send_step(blocks - 1)
 
+    def sent_rows(k, carry):
+        row = row_of(k)
+
+        for p in range(PIECES):
+            @pl.when((z < LINE - 1) & (row <= z))
+            def _():
+                z_copy(row, p, 0, z + 1).wait_send()
+
+            @pl.when((z > 0) & (row >= z))
+            def _():
+                z_copy(row, p, 1, z - 1).wait_send()
+
+            x_copy(row, x, p, 0).wait_send()
+            x_copy(row, x, p, 1).wait_send()
+
+        for p, q in zip(near, back):
+            far_copy(row, x_left, p, 0).wait_send()
+            far_copy(row, x_right, q, 1).wait_send()
+
+        return carry
+
+    lax.fori_loop(0, LINE, sent_rows, 0)
+
+    def sent_cot(i, carry):
+        cot_copy((d + i) % 16).wait_send()
+        return carry
+
+    lax.fori_loop(1, 16, sent_cot, 0)
+
     def out_copies(b):
         to = pl.ds(pl.multiple_of(b * tall, tall), tall)
         return (pltpu.make_async_copy(from_far.at[to], out.at[0, to], out_sem.at[b]),)
@@ -337,38 +373,17 @@
             from_twin[to, :].astype(jnp.float32) + from_far[to, :].astype(jnp.float32)
         )
         from_far[to, :] = mixed.astype(jnp.bfloat16)
-        for copy in out_copies(b):
-            copy.start()
+
+        @pl.when(b > 0)
+        def _():
+            for copy in out_copies(b - 1):
+                copy.start()
+
         return carry
 
     lax.fori_loop(0, blocks, mix, 0)
-
-    def sent_rows(k, carry):
-        row = row_of(k)
-
-        for p in range(PIECES):
-            @pl.when((z < LINE - 1) & (row <= z))
-            def _():
-                z_copy(row, p, 0, z + 1).wait_send()
-
-            @pl.when((z > 0) & (row >= z))
-            def _():
-                z_copy(row, p, 1, z - 1).wait_send()
-
-            x_copy(row, x, p, 0).wait_send()
-            x_copy(row, x, p, 1).wait_send()
-
-        far_copy(row, x_left, 0).wait_send()
-        far_copy(row, x_right, 1).wait_send()
-        return carry
-
-    lax.fori_loop(0, LINE, sent_rows, 0)
-
-    def sent_cot(i, carry):
-        cot_copy((d + i) % 16).wait_send()
-        return carry
-
-    lax.fori_loop(1, 16, sent_cot, 0)
+    for copy in out_copies(blocks - 1):
+        copy.start()
 
     def sent_blocks(b, carry):
         step_copy(b, 0).wait_send()
@@ -426,20 +441,21 @@
             scratch_shapes=[
                 pltpu.VMEM((count, width), jnp.bfloat16),
                 pltpu.VMEM((count, units), jnp.bfloat16),
+                pltpu.VMEM(hidden_grad.shape[1:], jnp.bfloat16),
                 pltpu.VMEM((width, wide), jnp.bfloat16),
                 pltpu.VMEM((count, wide), jnp.bfloat16),
                 pltpu.VMEM((tall, wide), jnp.float32),
                 pltpu.VMEM((width, wide), jnp.bfloat16),
                 pltpu.VMEM((width, wide), jnp.bfloat16),
                 pltpu.VMEM((width, wide), jnp.bfloat16),
-                dma((3,)),
+                dma((4,)),
                 dma(()),
                 dma((2, LINE, PIECES)),
                 dma((LINE, PIECES)),
                 dma((2, LINE, PIECES)),
                 dma((2, LINE, PIECES)),
-                dma((2, LINE)),
-                dma((2, LINE)),
+                dma((2, LINE, PIECES)),
+                dma((2, LINE, PIECES)),
                 dma((16,)),
                 dma((16,)),
                 dma((2, blocks)),
@@ -457,7 +473,7 @@
             out_shape=(out, out),
             in_specs=[pl.BlockSpec(memory_space=pl.ANY)],
             out_specs=(pl.BlockSpec(memory_space=pl.ANY),) * 2,
-            scratch_shapes=[pltpu.VMEM((width, wide), jnp.bfloat16), dma((blocks,)), dma((2, blocks))],
+            scratch_shapes=[pltpu.VMEM((width, wide), jnp.bfloat16), dma((4,)), dma((2, 4))],
             compiler_params=pltpu.CompilerParams(vmem_limit_bytes=60 * 1024 * 1024),
         )(mixed)
 

time: 217 us -> 216 us (level)
  no operation moved by 1% of the time
where the time goes in v4:
time: 216 us
  Pallas kernels  216 us (100%)
    pallas_call x1, Pallas kernels, local(): pl.pallas_call(functools.partial(kernel, groups), out_shape=jax.ShapeDtyp...  213 us

profile of v4, /device:TPU:32, one launch (start us, length us, event | category | flops | bytes accessed | tf_op | source)
XLA Modules:
  0.0 216.3 jit_solution(1563811987118470543)
XLA Ops:
  0.6 212.7 %shard_map.59.mixed = bf16[1,2048,768]{2,1,0:T(8,128)(2,1)} custom-call(bf16[1,128,2048]{2,1,0:T(8,128)(2,1)} %tokens.1, bf16[1,128,6144]{2,1,0:T(8,128)(2,1)} %hidden_grad.1, bf16[1,2048,384]{2,1,0:T(8,128)(2,1)} %w_gate.1, bf16[1,2048,384]{2,1,0:T(8,128)(2,1)} %w_up.1), custom_call_target="tpu_custom_call" | custom-call | tf_op jit(solution)/shard_map/pallas_call | solution.py:436
  213.4 2.9 %shard_map.60 = (bf16[1,2048,384]{2,1,0:T(8,128)(2,1)}, bf16[1,2048,384]{2,1,0:T(8,128)(2,1)}) custom-call(bf16[1,2048,768]{2,1,0:T(8,128)(2,1)} %shard_map.59.mixed), custom_call_target="tpu_custom_call" | custom-call | tf_op jit(solution)/shard_map/pallas_call | solution.py:471

commit v5 on v4

--- a/solution.py
+++ b/solution.py
@@ -50,14 +50,13 @@
 
     barrier = pltpu.get_barrier_semaphore()
 
-    def greet(i, carry):
-        peer = (d + i) % 16
-        pl.semaphore_signal(barrier, inc=1, device_id=(g, peer), device_id_type=MESH)
-        return carry
-
-    lax.fori_loop(1, 16, greet, 0)
-    pl.semaphore_signal(barrier, inc=1, device_id=(twin, d), device_id_type=MESH)
-    pl.semaphore_signal(barrier, inc=1, device_id=(far, d), device_id_type=MESH)
+    def greet(group, peer):
+        pl.semaphore_signal(barrier, inc=1, device_id=(group, peer), device_id_type=MESH)
+
+    greet(far, d)
+    for i in (8, 12, 4, 9, 11, 13, 7, 10, 6, 14, 5, 3, 15, 2, 1):
+        greet(g, (d + i) % 16)
+    greet(twin, d)
 
     def shard_at(row, col):
         return pl.ds(pl.multiple_of((row * LINE + col) * shard, shard), shard)

time: 216 us -> 216 us (level)
  no operation moved by 1% of the time
where the time goes in v5:
time: 216 us
  Pallas kernels  215 us (100%)
    pallas_call x1, Pallas kernels, local(): pl.pallas_call(functools.partial(kernel, groups), out_shape=jax.ShapeDtyp...  212 us

profile of v5, /device:TPU:32, one launch (start us, length us, event | category | flops | bytes accessed | tf_op | source)
XLA Modules:
  0.0 216.0 jit_solution(14836095971379997925)
XLA Ops:
  0.6 212.5 %shard_map.59.mixed = bf16[1,2048,768]{2,1,0:T(8,128)(2,1)} custom-call(bf16[1,128,2048]{2,1,0:T(8,128)(2,1)} %tokens.1, bf16[1,128,6144]{2,1,0:T(8,128)(2,1)} %hidden_grad.1, bf16[1,2048,384]{2,1,0:T(8,128)(2,1)} %w_gate.1, bf16[1,2048,384]{2,1,0:T(8,128)(2,1)} %w_up.1), custom_call_target="tpu_custom_call" | custom-call | tf_op jit(solution)/shard_map/pallas_call | solution.py:435
  213.1 2.9 %shard_map.60 = (bf16[1,2048,384]{2,1,0:T(8,128)(2,1)}, bf16[1,2048,384]{2,1,0:T(8,128)(2,1)}) custom-call(bf16[1,2048,768]{2,1,0:T(8,128)(2,1)} %shard_map.59.mixed), custom_call_target="tpu_custom_call" | custom-call | tf_op jit(solution)/shard_map/pallas_call | solution.py:470
